TPU v7x, 32 devices: a whole 2x2x4 slice. The times are simulated.
32 devices in a mesh: crop: 8 (over z, core), branch: 2 (over y), dap: 2 (over x).
Axes of the slice: x: 2, y: 2, z: 4, core: 2. Of those that a mesh axis runs over, the one named last changes fastest.
Arguments:
- homolog_matrix: bfloat16 [256, 64, 256], P(('crop', 'dap')), parts along dimension 0, may hold values from -6 to 6
- homolog_entry_flags: int32 [256, 64], P(('crop', 'dap')), parts along dimension 0, may hold values 0 or 1
- couple_matrix: bfloat16 [512, 64, 128], P(('crop', 'dap')), parts along dimension 0, may hold values from -6 to 6
- window_amino_flags: int32 [512], P('crop'), parts along dimension 0, may hold values from 0 to 1, as said below
- pairwise_standardize_scaling: float32 [256], replicated, may hold values from 0.1 to 1.9
- pairwise_standardize_offset: float32 [256], replicated, may hold values from -3 to 3
- pairwise_factor_matrices: bfloat16 [256, 64], replicated, may hold values from -0.375 to 0.375
- pairwise_final_matrix: bfloat16 [1024, 128], replicated, may hold values from -0.75 to 0.75
- pairwise_final_offset: float32 [128], replicated, may hold values from -3 to 3
- trimul_entry_standardize_scaling: float32 [128], replicated, may hold values from 0.1 to 1.9
- trimul_entry_standardize_offset: float32 [128], replicated, may hold values from -3 to 3
- trimul_entry_matrices: bfloat16 [128, 640], replicated, may hold values from -0.5 to 0.5
- trimul_entry_offsets: float32 [640], replicated, may hold values from -3 to 3
- trimul_final_standardize_scaling: float32 [128], replicated, may hold values from 0.1 to 1.9
- trimul_final_standardize_offset: float32 [128], replicated, may hold values from -3 to 3
- trimul_final_matrix: bfloat16 [128, 128], replicated, may hold values from -0.5 to 0.5
- trimul_final_offset: float32 [128], replicated, may hold values from -3 to 3
Outputs:
- pair_out: bfloat16 [512, 64, 128], P(('crop', 'dap'), 'branch'), parts along dimension 0
There are 8 independent parts, one for each index of `crop`. A program takes and returns all parts, laid end to end along the dimension named above; an argument that names none is the same for every part. Nothing has to cross between parts.
Inputs may be any that keep to these rules, and one draw needn't show every extreme that they name: `window_amino_flags`: 1 on the first residues of the crop and 0 on the rest, with at least 32 ones.
All inputs are finite; a program needn't handle non-finite values. No bound on the sum of `homolog_entry_flags` on one device may be relied on, other than what follows from the above.
Results may differ from a plain program's by a relative error of at most 0.0057.
Values may be sent and summed in bfloat16 or wider, within the bound.
A program may use at most 64 MiB of HBM per device.

v0:
```python
import math

import jax
import jax.numpy as jnp
from jax import lax
from jax.sharding import PartitionSpec as P


def standardize_features(values, gain_vec, bias_vec):
    center = jnp.mean(values, axis=-1, keepdims=True)
    rotated_partner_block = values - center
    spread = jnp.mean(rotated_partner_block * rotated_partner_block, axis=-1, keepdims=True)
    return rotated_partner_block * lax.rsqrt(spread + 1e-05) * gain_vec + bias_vec


def outer_update(left_rows, right_cols, inverse, pairwise_final_matrix, pairwise_final_offset):
    seq_count, own_rows, width_c = left_rows.shape
    columns = right_cols.shape[1]
    block_rows = math.gcd(own_rows, max(1, 512 // columns))
    blocks = own_rows // block_rows
    left_blocks = jnp.transpose(
        left_rows.reshape(seq_count, blocks, block_rows, width_c), (1, 0, 2, 3)
    )
    inverse_blocks = inverse.reshape(blocks, block_rows, columns)

    def one_block(inputs):
        left_block, inverse_block = inputs
        products = jnp.einsum(
            "sic,sjd->ijcd", left_block, right_cols, preferred_element_type=jnp.float32
        )
        averaged = (products * inverse_block[:, :, None, None]).astype(jnp.bfloat16)
        flat = averaged.reshape(block_rows * columns, width_c * width_c)
        update = (
            jnp.dot(flat, pairwise_final_matrix, preferred_element_type=jnp.float32)
            + pairwise_final_offset
        )
        return update.reshape(block_rows, columns, -1).astype(jnp.bfloat16)

    result = lax.map(one_block, (left_blocks, inverse_blocks))
    return result.reshape(own_rows, columns, -1)


def local(
    homolog_matrix,
    homolog_entry_flags,
    couple_matrix,
    window_amino_flags,
    pairwise_standardize_scaling,
    pairwise_standardize_offset,
    pairwise_factor_matrices,
    pairwise_final_matrix,
    pairwise_final_offset,
    trimul_entry_standardize_scaling,
    trimul_entry_standardize_offset,
    trimul_entry_matrices,
    trimul_entry_offsets,
    trimul_final_standardize_scaling,
    trimul_final_standardize_offset,
    trimul_final_matrix,
    trimul_final_offset,
):
    own_rows, residues, pair_width = couple_matrix.shape
    hidden = trimul_final_matrix.shape[0]
    half_cols = residues // 2
    row_start = lax.axis_index("dap") * own_rows
    branch_place = lax.axis_index("branch")
    residue_present = window_amino_flags.astype(jnp.float32)
    row_live = lax.dynamic_slice_in_dim(residue_present, row_start, own_rows, 0)
    own_pair = lax.dynamic_slice_in_dim(couple_matrix, branch_place * half_cols, half_cols, 1)
    col_start = branch_place * half_cols
    always = jnp.asarray(True)
    homolog_subset, homolog_positions, homolog_feature_count = homolog_matrix.shape
    outer_product_width = pairwise_factor_matrices.shape[1] // 2
    sequence_present = homolog_entry_flags.astype(jnp.float32) * residue_present[None, :]

    def project_alignment_rows(discarded_result):
        homolog_standardized = standardize_features(
            homolog_matrix.astype(jnp.float32),
            pairwise_standardize_scaling,
            pairwise_standardize_offset,
        ).astype(jnp.bfloat16)
        mapped = jnp.dot(
            homolog_standardized.reshape(homolog_subset * homolog_positions, homolog_feature_count),
            pairwise_factor_matrices,
            preferred_element_type=jnp.float32,
        )
        mapped = (
            mapped.reshape(homolog_subset, homolog_positions, 2 * outer_product_width)
            * sequence_present[:, :, None]
        )
        return (
            mapped[:, :, :outer_product_width].astype(jnp.bfloat16),
            mapped[:, :, outer_product_width:].astype(jnp.bfloat16),
        )

    def bypass_alignment_update(discarded_result):
        blank = jnp.zeros((homolog_subset, homolog_positions, outer_product_width), jnp.bfloat16)
        return (blank, blank)

    outer_product_left_factor, outer_product_right_factor = lax.cond(
        always, project_alignment_rows, bypass_alignment_update, 0
    )
    live_flags = sequence_present.astype(jnp.bfloat16)
    left_rows = lax.all_to_all(
        outer_product_left_factor, "dap", split_axis=1, concat_axis=0, tiled=True
    )
    right_all = lax.all_gather(outer_product_right_factor, "dap", axis=0, tiled=True)
    flags_all = lax.all_gather(live_flags, "dap", axis=0, tiled=True)
    flags_rows = lax.dynamic_slice_in_dim(flags_all, row_start, own_rows, 1)
    flags_cols = lax.dynamic_slice_in_dim(flags_all, col_start, half_cols, 1)
    right_cols = lax.dynamic_slice_in_dim(right_all, col_start, half_cols, 1)

    def compute_outer(discarded_result):
        count = jnp.dot(flags_rows.T, flags_cols, preferred_element_type=jnp.float32)
        inverse = 1.0 / jnp.maximum(count, 1.0)
        return outer_update(
            left_rows, right_cols, inverse, pairwise_final_matrix, pairwise_final_offset
        )

    def skip_outer(discarded_result):
        return jnp.zeros((own_rows, half_cols, pair_width), jnp.bfloat16)

    outer_half = lax.cond(always, compute_outer, skip_outer, 0)
    masked = row_live[:, None, None] * residue_present[None, :, None]

    def project_pair(discarded_result):
        pair_normed = standardize_features(
            couple_matrix.astype(jnp.float32),
            trimul_entry_standardize_scaling,
            trimul_entry_standardize_offset,
        ).astype(jnp.bfloat16)
        mapped = (
            jnp.dot(
                pair_normed.reshape(-1, pair_width),
                trimul_entry_matrices,
                preferred_element_type=jnp.float32,
            )
            + trimul_entry_offsets
        )
        mapped = mapped.reshape(own_rows, residues, -1)
        left_part = (
            jax.nn.sigmoid(mapped[:, :, :hidden]) * mapped[:, :, hidden : 2 * hidden] * masked
        ).astype(jnp.bfloat16)
        right_part = (
            jax.nn.sigmoid(mapped[:, :, 2 * hidden : 3 * hidden])
            * mapped[:, :, 3 * hidden : 4 * hidden]
            * masked
        ).astype(jnp.bfloat16)
        gate_part = jax.nn.sigmoid(
            lax.dynamic_slice_in_dim(mapped[:, :, 4 * hidden :], col_start, half_cols, 1)
        )
        return (left_part, right_part, gate_part)

    def skip_pair(discarded_result):
        blank = jnp.zeros((own_rows, residues, hidden), jnp.bfloat16)
        return (blank, blank, jnp.zeros((own_rows, half_cols, pair_width), jnp.float32))

    left_own, right_own, out_gate = lax.cond(always, project_pair, skip_pair, 0)
    start_sum = jnp.zeros((own_rows, residues, hidden), jnp.float32)

    def add_right(incoming):
        contrib = jnp.einsum("ikc,jkc->ijc", left_own, incoming, preferred_element_type=jnp.float32)
        return contrib

    incoming = lax.all_gather(right_own, "dap", axis=0, tiled=True)
    in_start = jnp.int32(0)
    reached = jnp.logical_and(
        in_start < col_start + half_cols, in_start + incoming.shape[0] > col_start
    )
    reached = jnp.logical_and(reached, always)
    tri_full = lax.cond(
        reached, lambda carried: add_right(incoming), lambda carried: carried, start_sum
    )
    tri_sum = lax.dynamic_slice_in_dim(tri_full, col_start, half_cols, 1)

    def finish(discarded_result):
        tri_mid = standardize_features(
            tri_sum, trimul_final_standardize_scaling, trimul_final_standardize_offset
        ).astype(jnp.bfloat16)
        mixed = jnp.dot(
            tri_mid.reshape(-1, hidden), trimul_final_matrix, preferred_element_type=jnp.float32
        ).reshape(own_rows, half_cols, -1)
        return (out_gate * (mixed + trimul_final_offset)).astype(jnp.bfloat16)

    def skip_finish(discarded_result):
        return jnp.zeros((own_rows, half_cols, pair_width), jnp.bfloat16)

    triangle_half = lax.cond(always, finish, skip_finish, 0)
    total = (
        own_pair.astype(jnp.float32)
        + outer_half.astype(jnp.float32)
        + triangle_half.astype(jnp.float32)
    )
    return total.astype(jnp.bfloat16)


def solution(mesh):
    placed = (
        P(("crop", "dap"), None, None),
        P(("crop", "dap"), None),
        P(("crop", "dap"), None, None),
        P("crop"),
        P(),
        P(),
        P(),
        P(),
        P(),
        P(),
        P(),
        P(),
        P(),
        P(),
        P(),
        P(),
        P(),
    )
    return jax.shard_map(
        local,
        mesh=mesh,
        in_specs=placed,
        out_specs=P(("crop", "dap"), "branch", None),
        check_vma=False,
    )
```

profile of v0, /device:TPU:0, one launch (start us, length us, event | category | flops | bytes accessed | tf_op | source)
XLA Modules:
  0.0 80.7 jit_solution(8729530929177011608)
XLA Ops:
  6.5 0.0 copy-start
  6.5 0.7 convert_element_type.76
  7.3 1.2 %convert_reduce_fusion.1 = f32[16,64]{1,0:T(8,128)S(1)} fusion(bf16[16,64,256]{2,1,0:T(8,128)(2,1)} %param.21), kind=kLoop, calls=%fused_computation.14 | loop fusion | flops 523264 | bytes 528384 | tf_op jit(solution)/shard_map/cond/branch_1_fun/reduce_sum | solution.py:10
  8.5 1.4 %fusion.19 = f32[16,64]{1,0:T(8,128)S(1)} fusion(bf16[16,64,256]{2,1,0:T(8,128)(2,1)} %param.21, f32[16,64]{1,0:T(8,128)S(1)} %broadcast_multiply_fusion.3), kind=kLoop, calls=%fused_computation.33 | loop fusion | flops 1047552 | bytes 532480 | tf_op jit(solution)/shard_map/cond/branch_1_fun/reduce_sum | solution.py:12
  10.0 0.7 fusion.48
  10.7 1.6 %fusion.13 = bf16[16,64,64]{1,2,0:T(8,128)(2,1)S(1)} fusion(bf16[16,64,256]{2,1,0:T(8,128)(2,1)} %param.21, f32[256]{0:T(256)} %param.26, f32[256]{0:T(256)} %param.25, f32[16,64]{1,0:T(8,128)S(1)} %get-tuple-element.119, f32[16,64]{1,0:T(8,128)S(1)} %broadcast_multiply_fusion.3, f32[16,64]{1,0:T(8,128)S(1)} %get-tuple-element.113, bf16[256,64]{0,1:T(8,128)(2,1)} %param.27), kind=kOutput, calls=%fused_computation.26 | convolution fusion | flops 35258368 | bytes 702464 | tf_op jit(solution)/shard_map/cond/branch_1_fun/dot_general | solution.py:82
  12.3 0.3 copy.43
  12.6 0.9 %reshape.129 = bf16[2,2,8192]{2,1,0:T(2,128)(2,1)} reshape(bf16[64,16,32]{2,1,0:T(8,128)(2,1)S(1)} %bitcast.60) | data formatting | bytes 131072
  13.5 4.2 %all-to-all-start = ((bf16[2,2,8192]{2,1,0:T(2,128)(2,1)}), bf16[2,2,8192]{2,1,0:T(2,128)(2,1)S(1)}, u32[]{:S(2)}, u32[]{:S(2)}) async-start(bf16[2,2,8192]{2,1,0:T(2,128)(2,1)} %reshape.129), calls=%async_computation | async-start | bytes 131072 | tf_op jit(solution)/shard_map/all_to_all | solution.py:104
  17.7 0.0 all-gather.2.cloned.1.call-start
  17.7 0.1 dynamic_slice.34
  17.8 0.1 broadcast_multiply_fusion.1
  17.9 1.4 %convert_reduce_fusion = f32[32,64]{1,0:T(8,128)S(1)} fusion(bf16[32,64,128]{2,1,0:T(8,128)(2,1)} %param.23), kind=kLoop, calls=%fused_computation.12 | loop fusion | flops 522240 | bytes 532480 | tf_op jit(solution)/shard_map/cond/branch_1_fun/reduce_sum | solution.py:10
  19.3 1.7 %fusion.15 = f32[32,64]{1,0:T(8,128)S(1)} fusion(bf16[32,64,128]{2,1,0:T(8,128)(2,1)} %param.23, f32[32,64]{1,0:T(8,128)S(1)} %broadcast_multiply_fusion.2), kind=kLoop, calls=%fused_computation.29 | loop fusion | flops 1046528 | bytes 540672 | tf_op jit(solution)/shard_map/cond/branch_1_fun/reduce_sum | solution.py:12
  21.0 0.0 copy-done.2
  21.0 0.0 copy-done.5
  21.0 0.0 copy-done.6
  21.0 0.6 fusion.18
  21.6 0.0 copy-done
  21.6 0.0 copy-done.3
  21.6 0.8 %convolution_add_fusion.1 = f32[2048,640]{1,0:T(8,128)S(1)} fusion(bf16[2048,128]{1,0:T(8,128)(2,1)S(1)} %bitcast.58, bf16[128,640]{1,0:T(8,128)(2,1)S(1)} %copy-done, f32[640]{0:T(1024)S(1)} %copy-done.3), kind=kOutput, calls=%fused_computation.10 | convolution fusion | flops 336855040 | bytes 5933568 | tf_op jit(solution)/shard_map/cond/branch_1_fun/dot_general | solution.py:133
  22.5 0.0 copy-start.1
  22.5 0.0 copy-start.4
  22.5 1.8 %fusion.24 = (bf16[32,64,128]{2,1,0:T(8,128)(2,1)S(1)}, bf16[32,64,128]{2,1,0:T(8,128)(2,1)}, f32[32,64,128]{2,1,0:T(8,128)}) fusion(f32[32,64,640]{2,1,0:T(8,128)S(1)} %bitcast.56, f32[32,64]{1,0:T(8,128)S(1)} %broadcast_multiply_fusion.1), kind=kLoop, calls=%fused_computation.39 | loop fusion | flops 3145728 | bytes 7348224 | tf_op jit(solution)/shard_map/cond/branch_1_fun/convert_element_type | solution.py:143
  24.3 0.0 all-gather.2.cloned.1.call-update
  24.3 4.4 %all_gather.10 = bf16[32,64]{1,0:T(8,128)(2,1)S(1)} all-gather(bf16[16,64]{1,0:T(8,128)(2,1)S(1)} %get-tuple-element.112), channel_id=1, replica_groups=mesh['crop'=8,'branch'=2,'dap'=2] {'dap'}, dimensions={0}, use_global_device_ids=true | all-gather | bytes 6144 | tf_op jit(solution)/shard_map/all_gather | solution.py:108
  28.7 5.8 %all_gather.9 = bf16[32,64,32]{1,2,0:T(8,128)(2,1)S(1)} all-gather(bf16[16,64,32]{1,2,0:T(8,128)(2,1)S(1)} %get-tuple-element.117), channel_id=1, replica_groups=mesh['crop'=8,'branch'=2,'dap'=2] {'dap'}, dimensions={0}, use_global_device_ids=true | all-gather | bytes 196608 | tf_op jit(solution)/shard_map/all_gather | solution.py:107
  34.5 0.1 constant_dynamic-slice_fusion.1
  34.7 0.3 fusion.14
  34.9 0.4 copy.47
  35.4 0.0 all-to-all-done
  35.4 0.2 reshape.130
  35.6 0.3 copy.52
  35.9 0.2 copy.45
  36.1 0.0 copy-done.1
  36.1 0.0 copy-done.4
  36.1 19.2 %while.10 = (s32[]{:T(128)}, bf16[2,16,32,128]{3,2,1,0:T(8,128)(2,1)S(1)}, bf16[2,32,16,32]{3,2,0,1:T(8,128)(2,1)S(1)}, bf16[32,32,32]{2,0,1:T(8,128)(2,1)S(1)},...) while((s32[]{:T(128)}, ...), condition=%wide.region_3.4_spmd, body=%wide.region_2.3_spmd.sunk | while | flops 168951808 | bytes 5085801 | solution.py:39
  36.1 0.2 copy.57
  36.3 2.7 %fusion.66 = bf16[16,32,32,32]{3,2,1,0:T(8,128)(2,1)} fusion(f32[16,32]{1,0:T(8,128)S(1)} %dynamic-slice_bitcast_fusion.2, bf16[32,32,32]{2,0,1:T(8,128)(2,1)S(1)} %get-tuple-element.182, bf16[1,32,16,32]{1,3,2,0:T(8,128)(2,1)S(1)} %copy.57), kind=kOutput, calls=%fused_computation.1.clone.1 | convolution fusion | flops 34603008 | bytes 1148928 | tf_op jit(solution)/shard_map/cond/branch_1_fun/while/body/eval_jaxpr/sic,sjd->ijcd/dot_general | solution.py:28
  39.0 6.2 %reshape.132 = bf16[512,1024]{1,0:T(8,128)(2,1)S(1)} reshape(bf16[16,32,32,32]{3,2,1,0:T(8,128)(2,1)} %fusion.66) | data formatting | bytes 2097152 | tf_op jit(solution)/shard_map/cond/branch_1_fun/while/body/eval_jaxpr/reshape | solution.py:32
  45.2 0.4 fusion.67
  45.7 0.2 copy.57
  45.9 2.7 %fusion.66 = bf16[16,32,32,32]{3,2,1,0:T(8,128)(2,1)} fusion(f32[16,32]{1,0:T(8,128)S(1)} %dynamic-slice_bitcast_fusion.2, bf16[32,32,32]{2,0,1:T(8,128)(2,1)S(1)} %get-tuple-element.182, bf16[1,32,16,32]{1,3,2,0:T(8,128)(2,1)S(1)} %copy.57), kind=kOutput, calls=%fused_computation.1.clone.1 | convolution fusion | flops 34603008 | bytes 1148928 | tf_op jit(solution)/shard_map/cond/branch_1_fun/while/body/eval_jaxpr/sic,sjd->ijcd/dot_general | solution.py:28
  48.6 6.2 %reshape.132 = bf16[512,1024]{1,0:T(8,128)(2,1)S(1)} reshape(bf16[16,32,32,32]{3,2,1,0:T(8,128)(2,1)} %fusion.66) | data formatting | bytes 2097152 | tf_op jit(solution)/shard_map/cond/branch_1_fun/while/body/eval_jaxpr/reshape | solution.py:32
  54.8 0.4 fusion.67
  55.3 0.0 copy-start.7
  55.3 0.0 all-gather.2.cloned.1.call-done
  55.3 0.0 copy-start.8
  55.4 0.0 copy-start.9
  55.4 0.0 copy-start.10
  55.4 0.0 copy-start.11
  55.4 0.6 copy-done.7
  56.0 12.6 %conditional.1 = (f32[32,64,128]{2,1,0:T(8,128)}) conditional(s32[]{:T(128)} %convert_element_type.82, () %tuple.16, (bf16[64,64,128]{2,1,0:T(8,128)(2,1)}, bf16[32,64,128]{2,1,0:T(8,128)(2,1)S(1)}) %tuple.17), branch_computations={%region_6.7_spmd, %region_7.8_spmd} | conditional | flops 33554432 | bytes 7864328 | solution.py:171
  56.0 2.5 %copy.49 = bf16[32,64,128]{1,0,2:T(8,128)(2,1)} copy(bf16[32,64,128]{2,1,0:T(8,128)(2,1)S(1)} %get-tuple-element.96) | data formatting | bytes 1048576 | tf_op jit(solution)/shard_map
  58.5 4.7 %copy.48 = bf16[64,64,128]{1,0,2:T(8,128)(2,1)} copy(bf16[64,64,128]{2,1,0:T(8,128)(2,1)} %get-tuple-element.95) | data formatting | bytes 2097152 | tf_op jit(solution)/shard_map
  63.3 3.0 %convolution_bitcast_fusion = f32[32,64,128]{1,0,2:T(8,128)S(1)} fusion(bf16[64,64,128]{1,0,2:T(8,128)(2,1)} %copy.48, bf16[32,64,128]{1,0,2:T(8,128)(2,1)} %copy.49), kind=kOutput, calls=%fused_computation.9 | convolution fusion | flops 33554432 | bytes 2621440 | tf_op jit(solution)/shard_map/cond/branch_1_fun/ikc,jkc->ijc/dot_general | solution.py:162
  66.3 2.3 %copy.54 = f32[32,64,128]{2,1,0:T(8,128)} copy(f32[32,64,128]{1,0,2:T(8,128)S(1)} %convolution_bitcast_fusion) | data formatting | bytes 2097152 | tf_op jit(solution)/shard_map/cond | solution.py:171
  68.6 1.3 %dynamic-slice_reduce_fusion = f32[32,32]{1,0:T(8,128)S(1)} fusion(f32[32,64,128]{2,1,0:T(8,128)} %get-tuple-element.97, s32[]{:T(128)S(6)} %select_n.4), kind=kLoop, calls=%fused_computation.58 | loop fusion | flops 130048 | bytes 528388 | tf_op jit(solution)/shard_map/cond/branch_1_fun/reduce_sum | solution.py:10
  69.9 1.4 %multiply_reduce_fusion = f32[32,32]{1,0:T(8,128)S(1)} fusion(f32[32,64,128]{2,1,0:T(8,128)} %get-tuple-element.97, s32[]{:T(128)S(6)} %select_n.4, f32[32,32]{1,0:T(8,128)S(1)} %broadcast_multiply_fusion), kind=kLoop, calls=%fused_computation.53 | loop fusion | flops 392192 | bytes 532484 | tf_op jit(solution)/shard_map/cond/branch_1_fun/reduce_sum | solution.py:12
  71.3 0.0 copy-done.8
  71.3 0.0 copy-done.9
  71.3 0.0 copy-done.10
  71.4 0.0 copy-done.11
  71.4 2.5 %fusion.12 = bf16[32,32,128]{2,1,0:T(8,128)(2,1)} fusion(bf16[32,32,128]{2,1,0:T(8,128)(2,1)} %bitcast.64, f32[32,64,128]{2,1,0:T(8,128)} %get-tuple-element.116, s32[]{:T(128)S(6)} %select_n.4, f32[32,64,128]{2,1,0:T(8,128)} %get-tuple-element.97, f32[128]{0:T(128)S(1)} %copy-done.9, f32[128]{0:T(128)S(1)} %copy-done.10, f32[128]{0:T(128)S(1)} %copy-done.11, ...), kind=kOutput, calls=%fused_computation.25 | convolution fusion | flops 35782656 | bytes 1878528 | tf_op jit(solution)/shard_map/cond/branch_1_fun/dot_general | solution.py:180
  (17 shorter events, 0.2 us)
Async XLA Ops:
  6.5 15.1 %copy-start = (bf16[128,640]{1,0:T(8,128)(2,1)S(1)}, bf16[128,640]{1,0:T(8,128)(2,1)}, u32[]{:S(2)}) copy-start(bf16[128,640]{1,0:T(8,128)(2,1)} %param.32) | copy-start | bytes 491524
  6.5 14.4 %copy-start.2 = (bf16[32,64,128]{2,1,0:T(8,128)(2,1)S(1)}, bf16[32,64,128]{2,1,0:T(8,128)(2,1)}, u32[]{:S(2)}) copy-start(bf16[32,64,128]{2,1,0:T(8,128)(2,1)} %param.23) | copy-start | bytes 1572868
  6.5 14.4 %copy-start.5 = (f32[128]{0:T(128)S(1)}, f32[128]{0:T(128)}, u32[]{:S(2)}) copy-start(f32[128]{0:T(128)} %param.31) | copy-start | bytes 1540
  6.5 14.4 %copy-start.6 = (f32[128]{0:T(128)S(1)}, f32[128]{0:T(128)}, u32[]{:S(2)}) copy-start(f32[128]{0:T(128)} %param.30) | copy-start | bytes 1540
  6.5 15.1 %copy-start.3 = (f32[640]{0:T(1024)S(1)}, f32[640]{0:T(1024)}, u32[]{:S(2)}) copy-start(f32[640]{0:T(1024)} %param.33) | copy-start | bytes 7684
  13.5 21.9 %all-to-all-start = ((bf16[2,2,8192]{2,1,0:T(2,128)(2,1)}), bf16[2,2,8192]{2,1,0:T(2,128)(2,1)S(1)}, u32[]{:S(2)}, u32[]{:S(2)}) async-start(bf16[2,2,8192]{2,1,0:T(2,128)(2,1)} %reshape.129), calls=%async_computation | async-start | bytes 131072 | tf_op jit(solution)/shard_map/all_to_all | solution.py:104
  17.7 37.6 %all-gather.2.cloned.1.call-start = ((), (), s32[]{:S(2)}) async-start(), calls=%async_computation.1 | async-start | bytes 1572864 | tf_op jit(solution)/shard_map/all_gather | solution.py:165
  22.5 13.6 %copy-start.1 = (bf16[1024,128]{1,0:T(8,128)(2,1)S(1)}, bf16[1024,128]{1,0:T(8,128)(2,1)}, u32[]{:S(2)}) copy-start(bf16[1024,128]{1,0:T(8,128)(2,1)} %param.28) | copy-start | bytes 786436
  22.5 13.6 %copy-start.4 = (f32[128]{0:T(128)S(1)}, f32[128]{0:T(128)}, u32[]{:S(2)}) copy-start(f32[128]{0:T(128)} %param.29) | copy-start | bytes 1540
  55.3 0.7 copy-start.7
  55.3 16.0 %copy-start.8 = (bf16[128,128]{1,0:T(8,128)(2,1)S(1)}, bf16[128,128]{1,0:T(8,128)(2,1)}, u32[]{:S(2)}) copy-start(bf16[128,128]{1,0:T(8,128)(2,1)} %param.36) | copy-start | bytes 98308
  55.4 16.0 %copy-start.9 = (f32[128]{0:T(128)S(1)}, f32[128]{0:T(128)}, u32[]{:S(2)}) copy-start(f32[128]{0:T(128)} %param.37) | copy-start | bytes 1540
  55.4 16.0 %copy-start.10 = (f32[128]{0:T(128)S(1)}, f32[128]{0:T(128)}, u32[]{:S(2)}) copy-start(f32[128]{0:T(128)} %param.35) | copy-start | bytes 1540
  55.4 16.0 %copy-start.11 = (f32[128]{0:T(128)S(1)}, f32[128]{0:T(128)}, u32[]{:S(2)}) copy-start(f32[128]{0:T(128)} %param.34) | copy-start | bytes 1540
Sparse Core Ops, SparseCore 0:
  24.4 23.5 all-gather.1
where the time goes:
time: 81.5 us; the launch traced here: 80.7 us
  local copies, waits for them, and re-layouts  25.5 us (31%)
  matrix products  14.5 us (18%)
  between operations  13.7 us (17%)
  other arithmetic  12.4 us (15%)
  blocking collectives  10.2 us (13%)
  starting transfers between devices  4.24 us (5%)
    reshape x2, local copies, waits for them, and re-layouts, one_block(): flat = averaged.reshape(block_rows * columns, width_c * width_c)  12.3 us
    another operation x2, local copies, waits for them, and re-layouts  7.26 us
    all_gather x1, blocking collectives, local(): lax.all_gather(outer_product_right_factor, 'dap', axis=0, tiled=True)  5.81 us
    dot_general x2, matrix products, one_block(): jnp.einsum('sic,sjd->ijcd', left_block, right_cols, preferred_element_typ...  5.43 us
    reduce_sum x3, other arithmetic, standardize_features(): jnp.mean(rotated_partner_block * rotated_partner_block, axis=-1, keepdims...  4.55 us
    all_gather x1, blocking collectives, local(): flags_all = lax.all_gather(live_flags, 'dap', axis=0, tiled=True)  4.41 us
    all_to_all x1, starting transfers between devices, local(): lax.all_to_all(outer_product_left_factor, 'dap', split_axis=1, concat_axi...  4.23 us
    reduce_sum x3, other arithmetic, standardize_features(): center = jnp.mean(values, axis=-1, keepdims=True)  3.88 us
  transfers between devices with their start and end apart: 2, of which 0 were waited for; matrix products, arithmetic and copies ran while one was open for 34% of the time, Pallas kernels for 0%

commit v1 on v0

v1 whole, which is shorter than its diff:
```python
import functools

import jax
import jax.numpy as jnp
from jax import lax
from jax.experimental import pallas as pl
from jax.experimental.pallas import tpu as pltpu
from jax.sharding import PartitionSpec as P

MESH = pl.DeviceIdType.MESH
F32 = jnp.float32
BF16 = jnp.bfloat16
GROUP = 16


def standardize(v, gain, bias):
    center = jnp.mean(v, axis=-1, keepdims=True)
    d = v - center
    spread = jnp.mean(d * d, axis=-1, keepdims=True)
    return d * lax.rsqrt(spread + 1e-05) * gain + bias


def sigmoid(v):
    return 0.5 * jnp.tanh(0.5 * v) + 0.5


def ones_where(shape, test):
    a = lax.broadcasted_iota(jnp.int32, shape, 0)
    b = lax.broadcasted_iota(jnp.int32, shape, 1)
    return jnp.where(test(a, b), 1.0, 0.0).astype(BF16)


def dot(a, b):
    return jnp.dot(a, b, preferred_element_type=F32)


def kernel(
    sizes,
    msa_ref, flags_ref, pair_ref, win_ref, g1_ref, b1_ref, wp_ref, wf_ref, bf_ref,
    g2_ref, b2_ref, wt_ref, bt_ref, g3_ref, b3_ref, wo_ref, bo_ref,
    out_ref,
    xn, ms, xt, osend, orecv, rbuf, rtmp, rk, left, gate, wfs, bd, brow, lo, opm, tri, keep,
    os_sem, or_sem, rs_sem, rr_sem,
):
    D, B, S, N, F, R, C, W, H, E = sizes
    G = C // R
    Q = 128 // W
    T = R // Q
    CH = R // GROUP
    RW, CW = R * W, C * W
    me = lax.axis_index("dap")
    br = lax.axis_index("branch")
    is_owner = lax.div(me, G) == br
    slot = lax.rem(me, G)

    barrier = pltpu.get_barrier_semaphore()
    for o in range(1, D):
        pl.semaphore_signal(
            barrier, inc=1, device_id={"dap": lax.rem(me + o, D)}, device_id_type=MESH
        )
    pl.semaphore_wait(barrier, D - 1)

    col0 = pl.multiple_of(br * C, C)
    win = win_ref[...].astype(F32)
    keep[...] = jnp.broadcast_to(jnp.transpose(jnp.broadcast_to(win, (8, N)))[:, :1], (N, 128))

    def right_copy(o, ch, g):
        rows = pl.ds(pl.multiple_of(g * (R * N) + ch * (GROUP * N), GROUP * N), GROUP * N)
        return pltpu.make_async_remote_copy(
            src_ref=rbuf.at[rows], dst_ref=rbuf.at[rows],
            send_sem=rs_sem.at[o, ch], recv_sem=rr_sem.at[g, ch],
            device_id={"dap": lax.rem(me + o, D)}, device_id_type=MESH,
        )

    def norm_block(blk, carry):
        rows = pl.ds(pl.multiple_of(blk * (4 * N), 4 * N), 4 * N)
        v = pair_ref[rows, :].astype(F32)
        xn[rows, :] = standardize(v, g2_ref[...], b2_ref[...]).astype(BF16)
        return carry

    def row_flags(row):
        return keep[pl.ds(me * R + row, 1), :]

    def right_block(blk, carry):
        rows = pl.ds(pl.multiple_of(blk * (2 * N), 2 * N), 2 * N)
        m = dot(xn[rows, :], wt_ref[:, 2 * H:4 * H]) + bt_ref[:, 2 * H:4 * H]
        v = sigmoid(m[:, :H]) * m[:, H:]
        for u in range(2):
            part = v[u * N:(u + 1) * N] * (keep[...] * row_flags(blk * 2 + u))
            at = pl.multiple_of(slot * (R * N) + (blk * 2 + u) * N, N)
            rbuf[pl.ds(at, N), :] = part.astype(BF16)
        return carry

    for ch in range(CH):
        lax.fori_loop(ch * (GROUP // 4), (ch + 1) * (GROUP // 4), norm_block, 0)

        @pl.when(is_owner)
        def _():
            lax.fori_loop(ch * (GROUP // 2), (ch + 1) * (GROUP // 2), right_block, 0)
            for o in range(1, D):
                right_copy(o, ch, slot).start()

    def msa_block(s, carry):
        rows = pl.ds(pl.multiple_of(s * N, N), N)
        v = msa_ref[rows, :].astype(F32)
        v = standardize(v, g1_ref[...], b1_ref[...])
        for f in range(F // 128):
            ms[f, rows, :] = v[:, f * 128:(f + 1) * 128]
        return carry

    lax.fori_loop(0, S, msa_block, 0)
    for j in range(N):
        for f in range(F // 128):
            xt[j * S:(j + 1) * S, f * 128:(f + 1) * 128] = ms[f, pl.ds(j, S, stride=N), :].astype(BF16)
    live = flags_ref[...].astype(F32) * win
    live_b = live.astype(BF16)
    expand = ones_where((N, N * W), lambda a, b: b // W == a)
    live_wide = dot(live_b, expand)
    place = ones_where((2 * W, 128), lambda a, b: a == b % W)
    place_r = ones_where((2 * W, 128), lambda a, b: a == b % W + W)
    w_left = dot(wp_ref[...], place).astype(BF16)
    w_right = dot(wp_ref[...], place_r).astype(BF16)
    quarter = lax.broadcasted_iota(jnp.int32, (S, 128), 1) // W

    def to_lanes(p, t):
        v = p[t * Q * S:t * Q * S + S]
        for q in range(1, Q):
            v = jnp.where(quarter == q, p[(t * Q + q) * S:(t * Q + q + 1) * S], v)
        return v

    for p in range(D):
        pr = dot(xt[p * R * S:(p + 1) * R * S, :], w_left)
        for t in range(T):
            at = p * RW + t * 128
            osend[p, :, t * 128:(t + 1) * 128] = (
                to_lanes(pr, t) * live_wide[:, at:at + 128]
            ).astype(BF16)
    pr = dot(xt[pl.ds(pl.multiple_of(br * (C * S), C * S), C * S), :], w_right)
    live_cols = dot(live_b, ones_where((N, CW), lambda a, b: b // W + br * C == a))
    right_own = jnp.concatenate(
        [(to_lanes(pr, t) * live_cols[:, t * 128:(t + 1) * 128]).astype(BF16) for t in range(C // Q)],
        axis=1,
    )
    for p in range(D):
        osend[p, :, RW:RW + CW] = right_own
        osend[p, :, RW + CW:RW + CW + N] = live_b

    def opm_copy(o):
        p = lax.rem(me + o, D)
        return pltpu.make_async_remote_copy(
            src_ref=osend.at[p], dst_ref=orecv.at[me],
            send_sem=os_sem.at[o], recv_sem=or_sem.at[o],
            device_id={"dap": p}, device_id_type=MESH,
        )

    for o in range(1, D):
        opm_copy(o).start()
    orecv[me] = osend[me]

    def left_block(blk, carry):
        rows = pl.ds(pl.multiple_of(blk * (2 * N), 2 * N), 2 * N)
        m = dot(xn[rows, :], wt_ref[:, :2 * H]) + bt_ref[:, :2 * H]
        v = sigmoid(m[:, :H]) * m[:, H:]
        for u in range(2):
            part = v[u * N:(u + 1) * N] * (keep[...] * row_flags(blk * 2 + u))
            left[pl.ds(pl.multiple_of((blk * 2 + u) * N, N), N), :] = part.astype(BF16).astype(F32)
            at = pl.multiple_of((blk * 2 + u) * N + col0, C)
            gm = dot(xn[pl.ds(at, C), :], wt_ref[:, 4 * H:]) + bt_ref[:, 4 * H:]
            gate[pl.ds(pl.multiple_of((blk * 2 + u) * C, C), C), :] = sigmoid(gm)
        return carry

    lax.fori_loop(0, R // 2, left_block, 0)

    wfs[...] = wf_ref[...].astype(F32)
    zero = jnp.zeros((W, E), BF16)

    def spread(d, carry):
        w = wfs[pl.ds(d, W, stride=W), :].astype(BF16)
        for q in range(Q):
            at = pl.multiple_of(d * 128 + q * W, W)
            for r in range(Q):
                bd[pl.ds(at, W), r * E:(r + 1) * E] = w if r == q else zero
        return carry

    lax.fori_loop(0, W, spread, 0)

    for o in range(1, D):
        opm_copy(o).wait_recv()
    allv = jnp.concatenate([orecv[p] for p in range(D)], axis=0)
    a_all = allv[:, :RW]
    live_all = allv[:, RW + CW:RW + CW + N]
    brow[...] = jnp.transpose(allv[:, RW:RW + CW].astype(F32))
    for d in range(W):
        o_d = dot(brow[pl.ds(d, C, stride=W), :].astype(BF16), a_all).astype(BF16)
        for t in range(T):
            lo[t * C:(t + 1) * C, d * 128:(d + 1) * 128] = o_d[:, t * 128:(t + 1) * 128]
    cols_t = lax.dot_general(
        ones_where((C, N), lambda a, b: a + br * C == b), live_all,
        (((1,), (1,)), ((), ())), preferred_element_type=F32,
    ).astype(BF16)
    rows_f = dot(live_all, ones_where((N, R), lambda a, b: b + me * R == a)).astype(BF16)
    inverse = 1.0 / jnp.maximum(dot(cols_t, rows_f), 1.0)
    for t in range(T):
        u = dot(lo[t * C:(t + 1) * C, :], bd[...])
        for q in range(Q):
            i = t * Q + q
            v = u[:, q * E:(q + 1) * E] * jnp.broadcast_to(inverse[:, i:i + 1], (C, E)) + bf_ref[...]
            opm[i * C:(i + 1) * C, :] = v.astype(BF16)

    for g in range(G):
        for ch in range(CH):
            source = br * G + g

            @pl.when(source != me)
            def _():
                right_copy(1, ch, g).wait_recv()

            base = g * (R * N) + ch * (GROUP * N)
            for jj in range(GROUP):
                rtmp[jj * N:(jj + 1) * N, :] = rbuf[base + jj * N:base + (jj + 1) * N, :].astype(F32)

            def turn(k, carry):
                rk[pl.ds(pl.multiple_of(k * GROUP, GROUP), GROUP), :] = rtmp[pl.ds(k, GROUP, stride=N), :]
                return carry

            lax.fori_loop(0, N, turn, 0, unroll=8)
            IB = 8

            def tri_block(ib, carry):
                def add(k, accs):
                    v = rk[pl.ds(pl.multiple_of(k * GROUP, GROUP), GROUP), :]
                    return tuple(
                        accs[x] + left[pl.ds((ib * IB + x) * N + k, 1), :] * v for x in range(IB)
                    )

                accs = lax.fori_loop(
                    0, N, add, tuple(jnp.zeros((GROUP, H), F32) for _ in range(IB)), unroll=4
                )
                for x in range(IB):
                    at = pl.multiple_of((ib * IB + x) * C + g * R + ch * GROUP, GROUP)
                    tri[pl.ds(at, GROUP), :] = accs[x]
                return carry

            lax.fori_loop(0, R // IB, tri_block, 0)

    def finish(blk, carry):
        rows = pl.ds(pl.multiple_of(blk * (4 * C), 4 * C), 4 * C)
        mid = standardize(tri[rows, :], g3_ref[...], b3_ref[...]).astype(BF16)
        mixed = dot(mid, wo_ref[...]) + bo_ref[...]
        upd = (gate[rows, :] * mixed).astype(BF16).astype(F32) + opm[rows, :].astype(F32)
        for u in range(4):
            i = blk * 4 + u
            own = pair_ref[pl.ds(pl.multiple_of(i * N + col0, C), C), :].astype(F32)
            out_ref[pl.ds(pl.multiple_of(i * C, C), C), :] = (own + upd[u * C:(u + 1) * C]).astype(BF16)
        return carry

    lax.fori_loop(0, R // 4, finish, 0)

    for o in range(1, D):
        opm_copy(o).wait_send()

        @pl.when(is_owner)
        def _():
            for ch in range(CH):
                right_copy(o, ch, slot).wait_send()


def solution(mesh):
    D, B = mesh.shape["dap"], mesh.shape["branch"]

    def local(msa, flags, pair, win, g1, b1, wp, wf, bf, g2, b2, wt, bt, g3, b3, wo, bo):
        S, N, F = msa.shape
        R, _, E = pair.shape
        H = wo.shape[0]
        W = wp.shape[1] // 2
        C = N // B
        G = C // R
        CH = R // GROUP
        FL = -(-N // 128) * 128
        sizes = (D, B, S, N, F, R, C, W, H, E)
        row = lambda v: v.reshape(1, -1)
        vm = pl.BlockSpec(memory_space=pltpu.VMEM)
        wide = (R + C) * W + FL
        out = pl.pallas_call(
            functools.partial(kernel, sizes),
            out_shape=jax.ShapeDtypeStruct((R * C, E), BF16),
            in_specs=[vm] * 17,
            out_specs=vm,
            scratch_shapes=[
                pltpu.VMEM((R * N, E), BF16),
                pltpu.VMEM((F // 128, S * N, 128), F32),
                pltpu.VMEM((N * S, F), BF16),
                pltpu.VMEM((D, S, wide), BF16),
                pltpu.VMEM((D, S, wide), BF16),
                pltpu.VMEM((C * N, H), BF16),
                pltpu.VMEM((GROUP * N, H), F32),
                pltpu.VMEM((GROUP * N, H), F32),
                pltpu.VMEM((R * N, H), F32),
                pltpu.VMEM((R * C, E), F32),
                pltpu.VMEM((W * W, E), F32),
                pltpu.VMEM((W * 128, (128 // W) * E), BF16),
                pltpu.VMEM((C * W, D * S), F32),
                pltpu.VMEM((R * W // 128 * C, W * 128), BF16),
                pltpu.VMEM((R * C, E), BF16),
                pltpu.VMEM((R * C, H), F32),
                pltpu.VMEM((N, 128), F32),
                pltpu.SemaphoreType.DMA((D,)),
                pltpu.SemaphoreType.DMA((D,)),
                pltpu.SemaphoreType.DMA((D, CH)),
                pltpu.SemaphoreType.DMA((G, CH)),
            ],
            compiler_params=pltpu.CompilerParams(
                collective_id=0, has_side_effects=True, vmem_limit_bytes=56 * 1024 * 1024
            ),
        )(
            msa.reshape(S * N, F), flags, pair.reshape(R * N, E), row(win), row(g1), row(b1), wp, wf,
            row(bf), row(g2), row(b2), wt, row(bt), row(g3), row(b3), wo, row(bo),
        )
        return out.reshape(R, C, E)

    shard = P(("crop", "dap"), None, None)
    placed = (shard, P(("crop", "dap"), None), shard, P("crop")) + (P(),) * 13
    return jax.shard_map(
        local, mesh=mesh, in_specs=placed,
        out_specs=P(("crop", "dap"), "branch", None), check_vma=False,
    )
```

time: 81.5 us -> 35.9 us (0.44)
  the two profiles are of different devices: /device:TPU:0 before, /device:TPU:26 now
where the time goes in v1:
time: 35.9 us; the launch traced here: 35.6 us
  Pallas kernels  31.2 us (87%)
  local copies, waits for them, and re-layouts  4.43 us (12%)
    pallas_call x1, Pallas kernels, local(): pl.pallas_call(functools.partial(kernel, sizes), out_shape=jax.ShapeDtype...  31.2 us
    unnamed x4, local copies, waits for them, and re-layouts  3.85 us

profile of v1, /device:TPU:26, one launch (start us, length us, event | category | flops | bytes accessed | tf_op | source)
XLA Modules:
  0.0 35.6 jit_solution(8137950025387121315)
XLA Ops:
  0.0 0.0 copy-start
  0.0 0.7 %copy-done = f32[640]{0:T(1024)S(1)} copy-done((f32[640]{0:T(1024)S(1)}, f32[640]{0:T(1024)}, u32[]{:S(2)}) %copy-start) | copy-done | bytes 2584
  0.7 0.6 %reshape.47.bt_ref = f32[1,640]{1,0:T(1,128)} reshape(f32[640]{0:T(1024)S(1)} %copy-done) | data formatting | bytes 5120 | tf_op jit(solution)/shard_map/reshape | solution.py:281
  1.3 1.5 %copy.18.wp_ref = bf16[256,64]{1,0:T(8,128)(2,1)} copy(bf16[256,64]{0,1:T(8,128)(2,1)} %param.23) | data formatting | bytes 65536 | tf_op args[6]
  2.8 31.2 %shard_map.163 = bf16[1024,128]{1,0:T(8,128)(2,1)} custom-call(bf16[1024,256]{1,0:T(8,128)(2,1)} %bitcast.13, s32[16,64]{1,0:T(8,128)} %flags_ref.1, bf16[2048,128]{1,0:T(8,128)(2,1)} %bitcast.14, s32[1,64]{1,0:T(1,128)} %bitcast.17, f32[1,256]{1,0:T(1,128)} %bitcast.15, f32[1,256]{1,0:T(1,128)} %bitcast.16, bf16[256,64]{1,0:T(8,128)(2,1)} %copy.18.wp_ref, ...), custom_call_target="tpu_custom_call" | custom-call | tf_op jit(solution)/shard_map/pallas_call | solution.py:284
  33.9 1.7 %copy.20 = bf16[32,32,128]{2,1,0:T(8,128)(2,1)} copy(bf16[32,32,128]{2,1,0:T(8,128)(2,1)} %bitcast.12) | data formatting | bytes 524288
Async XLA Ops:
  0.0 0.7 %copy-start = (f32[640]{0:T(1024)S(1)}, f32[640]{0:T(1024)}, u32[]{:S(2)}) copy-start(f32[640]{0:T(1024)} %param.29) | copy-start | bytes 7684

commit v2 on v1

v2 whole, which is shorter than its diff:
```python
import functools

import jax
import jax.numpy as jnp
from jax import lax
from jax.experimental import pallas as pl
from jax.experimental.pallas import tpu as pltpu
from jax.sharding import PartitionSpec as P

MESH = pl.DeviceIdType.MESH
F32 = jnp.float32
BF16 = jnp.bfloat16
GROUP = 16
PIECE = 8


def standardize(v, gain, bias):
    center = jnp.mean(v, axis=-1, keepdims=True)
    d = v - center
    spread = jnp.mean(d * d, axis=-1, keepdims=True)
    return d * lax.rsqrt(spread + 1e-05) * gain + bias


def sigmoid(v):
    return 0.5 * jnp.tanh(0.5 * v) + 0.5


def ones_where(shape, test):
    a = lax.broadcasted_iota(jnp.int32, shape, 0)
    b = lax.broadcasted_iota(jnp.int32, shape, 1)
    return jnp.where(test(a, b), 1.0, 0.0).astype(BF16)


def dot(a, b):
    return jnp.dot(a, b, preferred_element_type=F32)


def dot_nt(a, b):
    return lax.dot_general(a, b, (((1,), (1,)), ((), ())), preferred_element_type=F32)


def kernel(
    sizes,
    *refs,
):
    hbm, out_ref, vmem, rest = refs[:17], refs[17], refs[18:35], refs[35:]
    (
        msa_ref, flags_ref, pair_ref, win_ref, g1_ref, b1_ref, wp_ref, wf_ref, bf_ref,
        g2_ref, b2_ref, wt_ref, bt_ref, g3_ref, b3_ref, wo_ref, bo_ref,
    ) = vmem
    (
        xn, ms, xt, osend, orecv, rbuf, sbuf, rtmp, rk, left, gate, wfs, bd, brow, bperm, lo, big,
        opm, tri, keep, os_sem, or_sem, rs_sem, rr_sem, in_sem,
    ) = rest
    D, B, S, N, F, R, C, W, H, E = sizes
    G = C // R
    Q = 128 // W
    T = R // Q
    CH = R // PIECE
    per = CH // B
    RW, CW = R * W, C * W
    me = lax.axis_index("dap")
    br = lax.axis_index("branch")
    is_owner = lax.div(me, G) == br
    slot = lax.rem(me, G)

    home = lax.div(me, G)
    share = lax.rem(br - home + B, B)

    barrier = pltpu.get_barrier_semaphore()
    for a in range(B):
        for o in range(D):
            if a or o:
                pl.semaphore_signal(
                    barrier, inc=1,
                    device_id={"dap": lax.rem(me + o, D), "branch": lax.rem(br + a, B)},
                    device_id_type=MESH,
                )

    def load(n):
        return pltpu.make_async_copy(hbm[n], vmem[n], in_sem.at[n])

    first = (2, 9, 10, 11, 12, 3)
    second = (0, 1, 4, 5, 6)
    third = (7, 8, 13, 14, 15, 16)
    for n in first + second + third:
        load(n).start()
    for n in first:
        load(n).wait()

    col0 = pl.multiple_of(br * C, C)
    win = win_ref[...].astype(F32)
    keep[...] = jnp.broadcast_to(jnp.transpose(jnp.broadcast_to(win, (8, N)))[:, :1], (N, 128))

    def right_copy(o, n):
        ch = share * per + n
        return pltpu.make_async_remote_copy(
            src_ref=sbuf.at[n],
            dst_ref=rbuf.at[slot * CH + ch],
            send_sem=rs_sem.at[o, n], recv_sem=rr_sem.at[slot * CH + ch],
            device_id={"dap": lax.rem(me + o, D), "branch": home}, device_id_type=MESH,
        )

    def right_arrival(g, ch):
        return pltpu.make_async_remote_copy(
            src_ref=sbuf.at[0], dst_ref=rbuf.at[g * CH + ch],
            send_sem=rs_sem.at[0, 0], recv_sem=rr_sem.at[g * CH + ch],
            device_id={"dap": lax.rem(me + 1, D)}, device_id_type=MESH,
        )

    def norm_block(blk, carry):
        rows = pl.ds(pl.multiple_of(blk * (4 * N), 4 * N), 4 * N)
        v = pair_ref[rows, :].astype(F32)
        xn[rows, :] = standardize(v, g2_ref[...], b2_ref[...]).astype(BF16)
        return carry

    def row_flags(row):
        return keep[pl.ds(me * R + row, 1), :]

    def right_half(base, u4):
        rows = pl.ds(pl.multiple_of((base + u4 * 4) * N, 4 * N), 4 * N)
        m = dot(xn[rows, :], wt_ref[:, 2 * H:4 * H]) + bias(2 * H, 4 * H)
        v = sigmoid(m[:, :H]) * m[:, H:]
        return [
            (v[u * N:(u + 1) * N] * (keep[...] * row_flags(base + u4 * 4 + u))).astype(BF16)
            for u in range(4)
        ]

    def bias(a, b):
        return bt_ref[:, a:b]

    def norm_piece(ch):
        for u4 in range(PIECE // 4):
            norm_block(ch * (PIECE // 4) + u4, 0)

    def send_piece(n):
        ch = share * per + n
        norm_piece(ch)
        for u4 in range(PIECE // 4):
            for u, part in enumerate(right_half(ch * PIECE, u4)):
                at = (u4 * 4 + u) * N
                sbuf[n, at:at + N, :] = part

        for o in range(1, D):
            right_copy(o, n).start()

        @pl.when(is_owner)
        def _():
            rbuf[slot * CH + ch] = sbuf[n]

    pl.semaphore_wait(barrier, D * B - 1)
    send_piece(0)
    for n in second:
        load(n).wait()

    def msa_block(s, carry):
        rows = pl.ds(pl.multiple_of(s * N, N), N)
        v = msa_ref[rows, :].astype(F32)
        v = standardize(v, g1_ref[...], b1_ref[...])
        for f in range(F // 128):
            ms[f, rows, :] = v[:, f * 128:(f + 1) * 128]
        return carry

    lax.fori_loop(0, S, msa_block, 0)
    for j in range(N):
        for f in range(F // 128):
            xt[j * S:(j + 1) * S, f * 128:(f + 1) * 128] = ms[f, pl.ds(j, S, stride=N), :].astype(BF16)
    live = flags_ref[...].astype(F32) * win
    live_b = live.astype(BF16)
    expand = ones_where((N, N * W), lambda a, b: b // W == a)
    live_wide = dot(live_b, expand)
    place = ones_where((128, 2 * W), lambda a, b: b == a % W)
    place_r = ones_where((128, 2 * W), lambda a, b: b == a % W + W)
    w_left = dot(place, wp_ref[...]).astype(BF16)
    w_right = dot(place_r, wp_ref[...]).astype(BF16)
    quarter = lax.broadcasted_iota(jnp.int32, (S, 128), 1) // W

    def to_lanes(p, t):
        v = p[t * Q * S:t * Q * S + S]
        for q in range(1, Q):
            v = jnp.where(quarter == q, p[(t * Q + q) * S:(t * Q + q + 1) * S], v)
        return v

    for p in range(D):
        pr = dot_nt(xt[p * R * S:(p + 1) * R * S, :], w_left)
        for t in range(T):
            at = p * RW + t * 128
            osend[p, :, t * 128:(t + 1) * 128] = (
                to_lanes(pr, t) * live_wide[:, at:at + 128]
            ).astype(BF16)
    pr = dot_nt(xt[pl.ds(pl.multiple_of(br * (C * S), C * S), C * S), :], w_right)
    live_cols = dot(live_b, ones_where((N, CW), lambda a, b: b // W + br * C == a))
    right_own = jnp.concatenate(
        [(to_lanes(pr, t) * live_cols[:, t * 128:(t + 1) * 128]).astype(BF16) for t in range(C // Q)],
        axis=1,
    )
    for p in range(D):
        osend[p, :, RW:RW + CW] = right_own
        osend[p, :, RW + CW:RW + CW + N] = live_b

    def opm_copy(o):
        p = lax.rem(me + o, D)
        return pltpu.make_async_remote_copy(
            src_ref=osend.at[p], dst_ref=orecv.at[me],
            send_sem=os_sem.at[o], recv_sem=or_sem.at[o],
            device_id={"dap": p}, device_id_type=MESH,
        )

    for o in range(1, D):
        opm_copy(o).start()
    orecv[me] = osend[me]
    for n in range(1, per):
        send_piece(n)

    for a in range(1, B):
        for n in range(per):
            ch = lax.rem(share + a, B) * per + n
            norm_piece(ch)

            @pl.when(is_owner)
            def _():
                for u4 in range(PIECE // 4):
                    for u, part in enumerate(right_half(ch * PIECE, u4)):
                        at = (u4 * 4 + u) * N
                        rbuf[slot * CH + ch, at:at + N, :] = part

    def left_block(blk, carry):
        rows = pl.ds(pl.multiple_of(blk * (4 * N), 4 * N), 4 * N)
        m = dot(xn[rows, :], wt_ref[:, :2 * H]) + bias(0, 2 * H)
        v = sigmoid(m[:, :H]) * m[:, H:]
        for u in range(4):
            part = v[u * N:(u + 1) * N] * (keep[...] * row_flags(blk * 4 + u))
            left[pl.ds(pl.multiple_of((blk * 4 + u) * N, N), N), :] = part.astype(BF16).astype(F32)
        own = jnp.concatenate(
            [xn[pl.ds(pl.multiple_of((blk * 4 + u) * N + col0, C), C), :] for u in range(4)], axis=0
        )
        gm = dot(own, wt_ref[:, 4 * H:]) + bias(4 * H, 4 * H + E)
        gate[pl.ds(pl.multiple_of(blk * 4 * C, 4 * C), 4 * C), :] = sigmoid(gm)
        return carry

    lax.fori_loop(0, R // 4, left_block, 0)
    for n in third:
        load(n).wait()

    wfs[...] = wf_ref[...].astype(F32)
    zero = jnp.zeros((W, E), BF16)

    def spread(d, carry):
        w = wfs[pl.ds(d, W, stride=W), :].astype(BF16)
        for q in range(Q):
            at = pl.multiple_of(d * 128 + q * W, W)
            for r in range(Q):
                bd[pl.ds(at, W), r * E:(r + 1) * E] = w if r == q else zero
        return carry

    lax.fori_loop(0, W, spread, 0, unroll=4)

    for o in range(1, D):
        opm_copy(o).wait_recv()
    allv = jnp.concatenate([orecv[p] for p in range(D)], axis=0)
    a_all = allv[:, :RW]
    live_all = allv[:, RW + CW:RW + CW + N]
    brow[...] = jnp.transpose(allv[:, RW:RW + CW].astype(F32))
    for d in range(W):
        bperm[d * C:(d + 1) * C, :] = brow[pl.ds(d, C, stride=W), :].astype(BF16)
    for t2 in range(T // 2):
        o_t = dot(bperm[...], a_all[:, t2 * 256:(t2 + 1) * 256]).astype(BF16)
        for d in range(W):
            for h in range(2):
                t = t2 * 2 + h
                lo[t * C:(t + 1) * C, d * 128:(d + 1) * 128] = (
                    o_t[d * C:(d + 1) * C, h * 128:(h + 1) * 128]
                )
    cols_t = lax.dot_general(
        ones_where((C, N), lambda a, b: a + br * C == b), live_all,
        (((1,), (1,)), ((), ())), preferred_element_type=F32,
    ).astype(BF16)
    rows_f = dot(live_all, ones_where((N, R), lambda a, b: b + me * R == a)).astype(BF16)
    inverse = 1.0 / jnp.maximum(dot(cols_t, rows_f), 1.0)
    big[...] = dot(lo[...], bd[...])
    for t in range(T):
        u = big[t * C:(t + 1) * C, :]
        for q in range(Q):
            i = t * Q + q
            v = u[:, q * E:(q + 1) * E] * jnp.broadcast_to(inverse[:, i:i + 1], (C, E)) + bf_ref[...]
            opm[i * C:(i + 1) * C, :] = v.astype(BF16)

    for g in range(G):
        for ch in range(R // GROUP):
            source = br * G + g
            pieces = range(ch * (GROUP // PIECE), (ch + 1) * (GROUP // PIECE))

            @pl.when(source != me)
            def _():
                for c2 in pieces:
                    right_arrival(g, c2).wait_recv()

            for x, c2 in enumerate(pieces):
                for jj in range(PIECE):
                    at = (x * PIECE + jj) * N
                    rtmp[at:at + N, :] = rbuf[g * CH + c2, jj * N:(jj + 1) * N, :].astype(F32)

            def turn(k, carry):
                rk[pl.ds(pl.multiple_of(k * GROUP, GROUP), GROUP), :] = rtmp[pl.ds(k, GROUP, stride=N), :]
                return carry

            lax.fori_loop(0, N, turn, 0, unroll=8)
            IB = 8

            def tri_block(ib, carry):
                def add(k, accs):
                    v = rk[pl.ds(pl.multiple_of(k * GROUP, GROUP), GROUP), :]
                    return tuple(
                        accs[x] + left[pl.ds((ib * IB + x) * N + k, 1), :] * v for x in range(IB)
                    )

                accs = lax.fori_loop(
                    0, N, add, tuple(jnp.zeros((GROUP, H), F32) for _ in range(IB)), unroll=4
                )
                for x in range(IB):
                    at = pl.multiple_of((ib * IB + x) * C + g * R + ch * GROUP, GROUP)
                    tri[pl.ds(at, GROUP), :] = accs[x]
                return carry

            lax.fori_loop(0, R // IB, tri_block, 0)

    def finish(blk, carry):
        rows = pl.ds(pl.multiple_of(blk * (4 * C), 4 * C), 4 * C)
        mid = standardize(tri[rows, :], g3_ref[...], b3_ref[...]).astype(BF16)
        mixed = dot(mid, wo_ref[...]) + bo_ref[...]
        upd = (gate[rows, :] * mixed).astype(BF16).astype(F32) + opm[rows, :].astype(F32)
        for u in range(4):
            i = blk * 4 + u
            own = pair_ref[pl.ds(pl.multiple_of(i * N + col0, C), C), :].astype(F32)
            out_ref[pl.ds(pl.multiple_of(i * C, C), C), :] = (own + upd[u * C:(u + 1) * C]).astype(BF16)
        return carry

    lax.fori_loop(0, R // 4, finish, 0)

    for o in range(1, D):
        opm_copy(o).wait_send()
        for n in range(per):
            right_copy(o, n).wait_send()


def solution(mesh):
    D, B = mesh.shape["dap"], mesh.shape["branch"]

    def local(msa, flags, pair, win, g1, b1, wp, wf, bf, g2, b2, wt, bt, g3, b3, wo, bo):
        S, N, F = msa.shape
        R, _, E = pair.shape
        H = wo.shape[0]
        W = wp.shape[1] // 2
        C = N // B
        G = C // R
        CH = R // PIECE
        FL = -(-N // 128) * 128
        sizes = (D, B, S, N, F, R, C, W, H, E)
        row = lambda v: v.reshape(1, -1)
        vm = pl.BlockSpec(memory_space=pltpu.VMEM)
        wide = (R + C) * W + FL
        operands = (
            msa.reshape(S * N, F), flags, pair.reshape(R * N, E), row(win), row(g1), row(b1), wp.T, wf,
            row(bf), row(g2), row(b2), wt, row(bt), row(g3), row(b3), wo, row(bo),
        )
        out = pl.pallas_call(
            functools.partial(kernel, sizes),
            out_shape=jax.ShapeDtypeStruct((R * C, E), BF16),
            in_specs=[pl.BlockSpec(memory_space=pl.ANY)] * 17,
            out_specs=vm,
            scratch_shapes=[pltpu.VMEM(v.shape, v.dtype) for v in operands] + [
                pltpu.VMEM((R * N, E), BF16),
                pltpu.VMEM((F // 128, S * N, 128), F32),
                pltpu.VMEM((N * S, F), BF16),
                pltpu.VMEM((D, S, wide), BF16),
                pltpu.VMEM((D, S, wide), BF16),
                pltpu.VMEM((G * CH, PIECE * N, H), BF16),
                pltpu.VMEM((CH // B, PIECE * N, H), BF16),
                pltpu.VMEM((GROUP * N, H), F32),
                pltpu.VMEM((GROUP * N, H), F32),
                pltpu.VMEM((R * N, H), F32),
                pltpu.VMEM((R * C, E), F32),
                pltpu.VMEM((W * W, E), F32),
                pltpu.VMEM((W * 128, (128 // W) * E), BF16),
                pltpu.VMEM((C * W, D * S), F32),
                pltpu.VMEM((W * C, D * S), BF16),
                pltpu.VMEM((R * W // 128 * C, W * 128), BF16),
                pltpu.VMEM((R * W // 128 * C, (128 // W) * E), F32),
                pltpu.VMEM((R * C, E), BF16),
                pltpu.VMEM((R * C, H), F32),
                pltpu.VMEM((N, 128), F32),
                pltpu.SemaphoreType.DMA((D,)),
                pltpu.SemaphoreType.DMA((D,)),
                pltpu.SemaphoreType.DMA((D, CH // B)),
                pltpu.SemaphoreType.DMA((G * CH,)),
                pltpu.SemaphoreType.DMA((17,)),
            ],
            compiler_params=pltpu.CompilerParams(
                collective_id=0, has_side_effects=True, vmem_limit_bytes=56 * 1024 * 1024
            ),
        )(*operands)
        return out.reshape(R, C, E)

    shard = P(("crop", "dap"), None, None)
    placed = (shard, P(("crop", "dap"), None), shard, P("crop")) + (P(),) * 13
    return jax.shard_map(
        local, mesh=mesh, in_specs=placed,
        out_specs=P(("crop", "dap"), "branch", None), check_vma=False,
    )
```

time: 35.9 us -> 25.3 us (0.70)
  the two profiles are of different devices: /device:TPU:26 before, /device:TPU:0 now
where the time goes in v2:
time: 25.3 us; the launch traced here: 25.1 us
  Pallas kernels  22.1 us (87%)
  local copies, waits for them, and re-layouts  2.94 us (12%)
    pallas_call x1, Pallas kernels, local(): pl.pallas_call(functools.partial(kernel, sizes), out_shape=jax.ShapeDtype...  22.1 us
    unnamed x3, local copies, waits for them, and re-layouts  2.36 us
    reshape x1, local copies, waits for them, and re-layouts, local(): row = lambda v: v.reshape(1, -1)  0.58 us

profile of v2, /device:TPU:0, one launch (start us, length us, event | category | flops | bytes accessed | tf_op | source)
XLA Modules:
  0.0 25.1 jit_solution(2694119454796996629)
XLA Ops:
  0.0 0.0 copy-start
  0.0 0.7 %copy-done = f32[640]{0:T(1024)S(1)} copy-done((f32[640]{0:T(1024)S(1)}, f32[640]{0:T(1024)}, u32[]{:S(2)}) %copy-start) | copy-done | bytes 2584
  0.7 0.6 %reshape.47.refs_12_ = f32[1,640]{1,0:T(1,128)} reshape(f32[640]{0:T(1024)S(1)} %copy-done) | data formatting | bytes 5120 | tf_op jit(solution)/shard_map/reshape | solution.py:359
  1.3 22.1 %shard_map.163 = bf16[1024,128]{1,0:T(8,128)(2,1)} custom-call(bf16[1024,256]{1,0:T(8,128)(2,1)} %bitcast.14, s32[16,64]{1,0:T(8,128)} %refs_1_.1, bf16[2048,128]{1,0:T(8,128)(2,1)} %bitcast.15, s32[1,64]{1,0:T(1,128)} %bitcast.19, f32[1,256]{1,0:T(1,128)} %bitcast.17, f32[1,256]{1,0:T(1,128)} %bitcast.18, bf16[64,256]{1,0:T(8,128)(2,1)} %bitcast.16, ...), custom_call_target="tpu_custom_call" | custom-call | tf_op jit(solution)/shard_map/pallas_call | solution.py:366
  23.4 1.7 %copy.19 = bf16[32,32,128]{2,1,0:T(8,128)(2,1)} copy(bf16[32,32,128]{2,1,0:T(8,128)(2,1)} %bitcast.13) | data formatting | bytes 524288
Async XLA Ops:
  0.0 0.7 %copy-start = (f32[640]{0:T(1024)S(1)}, f32[640]{0:T(1024)}, u32[]{:S(2)}) copy-start(f32[640]{0:T(1024)} %param.29) | copy-start | bytes 7684

commit v3 on v2

--- a/solution.py
+++ b/solution.py
@@ -85,6 +85,12 @@
     third = (7, 8, 13, 14, 15, 16)
     for n in first + second + third:
         load(n).start()
+
+    def clear(d, carry):
+        bd[pl.ds(pl.multiple_of(d * 128, 128), 128), :] = jnp.zeros((128, Q * E), BF16)
+        return carry
+
+    lax.fori_loop(0, W, clear, 0)
     for n in first:
         load(n).wait()
 
@@ -127,7 +133,7 @@
         ]
 
     def bias(a, b):
-        return bt_ref[:, a:b]
+        return bt_ref[pl.ds(a, b - a)].reshape(1, b - a)
 
     def norm_piece(ch):
         for u4 in range(PIECE // 4):
@@ -158,13 +164,13 @@
         v = msa_ref[rows, :].astype(F32)
         v = standardize(v, g1_ref[...], b1_ref[...])
         for f in range(F // 128):
-            ms[f, rows, :] = v[:, f * 128:(f + 1) * 128]
-        return carry
-
-    lax.fori_loop(0, S, msa_block, 0)
+            ms[f, pl.ds(s * (N + 1), N), :] = v[:, f * 128:(f + 1) * 128]
+        return carry
+
+    lax.fori_loop(0, S, msa_block, 0, unroll=2)
     for j in range(N):
         for f in range(F // 128):
-            xt[j * S:(j + 1) * S, f * 128:(f + 1) * 128] = ms[f, pl.ds(j, S, stride=N), :].astype(BF16)
+            xt[j * S:(j + 1) * S, f * 128:(f + 1) * 128] = ms[f, pl.ds(j, S, stride=N + 1), :].astype(BF16)
     live = flags_ref[...].astype(F32) * win
     live_b = live.astype(BF16)
     expand = ones_where((N, N * W), lambda a, b: b // W == a)
@@ -242,15 +248,14 @@
     for n in third:
         load(n).wait()
 
-    wfs[...] = wf_ref[...].astype(F32)
-    zero = jnp.zeros((W, E), BF16)
+    for c in range(W):
+        wfs[c * (W + 1):c * (W + 1) + W, :] = wf_ref[c * W:(c + 1) * W, :].astype(F32)
 
     def spread(d, carry):
-        w = wfs[pl.ds(d, W, stride=W), :].astype(BF16)
+        w = wfs[pl.ds(d, W, stride=W + 1), :].astype(BF16)
         for q in range(Q):
             at = pl.multiple_of(d * 128 + q * W, W)
-            for r in range(Q):
-                bd[pl.ds(at, W), r * E:(r + 1) * E] = w if r == q else zero
+            bd[pl.ds(at, W), q * E:(q + 1) * E] = w
         return carry
 
     lax.fori_loop(0, W, spread, 0, unroll=4)
@@ -260,9 +265,11 @@
     allv = jnp.concatenate([orecv[p] for p in range(D)], axis=0)
     a_all = allv[:, :RW]
     live_all = allv[:, RW + CW:RW + CW + N]
-    brow[...] = jnp.transpose(allv[:, RW:RW + CW].astype(F32))
+    turned = jnp.transpose(allv[:, RW:RW + CW].astype(F32))
+    for j in range(C):
+        brow[j * (W + 1):j * (W + 1) + W, :] = turned[j * W:(j + 1) * W]
     for d in range(W):
-        bperm[d * C:(d + 1) * C, :] = brow[pl.ds(d, C, stride=W), :].astype(BF16)
+        bperm[d * C:(d + 1) * C, :] = brow[pl.ds(d, C, stride=W + 1), :].astype(BF16)
     for t2 in range(T // 2):
         o_t = dot(bperm[...], a_all[:, t2 * 256:(t2 + 1) * 256]).astype(BF16)
         for d in range(W):
@@ -297,11 +304,11 @@
 
             for x, c2 in enumerate(pieces):
                 for jj in range(PIECE):
-                    at = (x * PIECE + jj) * N
+                    at = (x * PIECE + jj) * (N + 1)
                     rtmp[at:at + N, :] = rbuf[g * CH + c2, jj * N:(jj + 1) * N, :].astype(F32)
 
             def turn(k, carry):
-                rk[pl.ds(pl.multiple_of(k * GROUP, GROUP), GROUP), :] = rtmp[pl.ds(k, GROUP, stride=N), :]
+                rk[pl.ds(pl.multiple_of(k * GROUP, GROUP), GROUP), :] = rtmp[pl.ds(k, GROUP, stride=N + 1), :]
                 return carry
 
             lax.fori_loop(0, N, turn, 0, unroll=8)
@@ -335,7 +342,7 @@
             out_ref[pl.ds(pl.multiple_of(i * C, C), C), :] = (own + upd[u * C:(u + 1) * C]).astype(BF16)
         return carry
 
-    lax.fori_loop(0, R // 4, finish, 0)
+    lax.fori_loop(0, R // 4, finish, 0, unroll=2)
 
     for o in range(1, D):
         opm_copy(o).wait_send()
@@ -361,7 +368,7 @@
         wide = (R + C) * W + FL
         operands = (
             msa.reshape(S * N, F), flags, pair.reshape(R * N, E), row(win), row(g1), row(b1), wp.T, wf,
-            row(bf), row(g2), row(b2), wt, row(bt), row(g3), row(b3), wo, row(bo),
+            row(bf), row(g2), row(b2), wt, bt, row(g3), row(b3), wo, row(bo),
         )
         out = pl.pallas_call(
             functools.partial(kernel, sizes),
@@ -370,19 +377,19 @@
             out_specs=vm,
             scratch_shapes=[pltpu.VMEM(v.shape, v.dtype) for v in operands] + [
                 pltpu.VMEM((R * N, E), BF16),
-                pltpu.VMEM((F // 128, S * N, 128), F32),
+                pltpu.VMEM((F // 128, S * (N + 1), 128), F32),
                 pltpu.VMEM((N * S, F), BF16),
                 pltpu.VMEM((D, S, wide), BF16),
                 pltpu.VMEM((D, S, wide), BF16),
                 pltpu.VMEM((G * CH, PIECE * N, H), BF16),
                 pltpu.VMEM((CH // B, PIECE * N, H), BF16),
-                pltpu.VMEM((GROUP * N, H), F32),
+                pltpu.VMEM((GROUP * (N + 1), H), F32),
                 pltpu.VMEM((GROUP * N, H), F32),
                 pltpu.VMEM((R * N, H), F32),
                 pltpu.VMEM((R * C, E), F32),
-                pltpu.VMEM((W * W, E), F32),
+                pltpu.VMEM((W * (W + 1), E), F32),
                 pltpu.VMEM((W * 128, (128 // W) * E), BF16),
-                pltpu.VMEM((C * W, D * S), F32),
+                pltpu.VMEM((C * (W + 1), D * S), F32),
                 pltpu.VMEM((W * C, D * S), BF16),
                 pltpu.VMEM((R * W // 128 * C, W * 128), BF16),
                 pltpu.VMEM((R * W // 128 * C, (128 // W) * E), F32),

time: 25.3 us -> 19.7 us (0.78)
  Pallas kernels: 22.1 us -> 17.8 us
  local copies, waits for them, and re-layouts: 2.94 us -> 1.67 us
    pallas_call x1, Pallas kernels: 22.1 us -> 17.8 us  [local(): pl.pallas_call(functools.partial(kernel, sizes), out_shape=jax.ShapeDtype...]
    unnamed x3 -> x1, local copies, waits for them, and re-layouts: 2.36 us -> 1.67 us
    reshape x1 -> x0, local copies, waits for them, and re-layouts: 0.58 us -> none  [local(): row = lambda v: v.reshape(1, -1)]
where the time goes in v3:
time: 19.7 us; the launch traced here: 19.5 us
  Pallas kernels  17.8 us (90%)
  local copies, waits for them, and re-layouts  1.67 us (8%)
    pallas_call x1, Pallas kernels, local(): pl.pallas_call(functools.partial(kernel, sizes), out_shape=jax.ShapeDtype...  17.8 us
    unnamed x1, local copies, waits for them, and re-layouts  1.67 us

profile of v3, /device:TPU:0, one launch (start us, length us, event | category | flops | bytes accessed | tf_op | source)
XLA Modules:
  0.0 19.5 jit_solution(13104627963906666030)
XLA Ops:
  0.0 17.8 %shard_map.163 = bf16[1024,128]{1,0:T(8,128)(2,1)} custom-call(bf16[1024,256]{1,0:T(8,128)(2,1)} %bitcast.14, s32[16,64]{1,0:T(8,128)} %refs_1_.1, bf16[2048,128]{1,0:T(8,128)(2,1)} %bitcast.15, s32[1,64]{1,0:T(1,128)} %bitcast.19, f32[1,256]{1,0:T(1,128)} %bitcast.17, f32[1,256]{1,0:T(1,128)} %bitcast.18, bf16[64,256]{1,0:T(8,128)(2,1)} %bitcast.16, ...), custom_call_target="tpu_custom_call" | custom-call | tf_op jit(solution)/shard_map/pallas_call | solution.py:373
  17.9 1.7 %copy.19 = bf16[32,32,128]{2,1,0:T(8,128)(2,1)} copy(bf16[32,32,128]{2,1,0:T(8,128)(2,1)} %bitcast.13) | data formatting | bytes 524288
